TPU v7x, 32 devices: a whole 2x2x4 slice. The times are simulated.
32 devices in a mesh: group: 2 (over y), seq: 4 (over z), tensor: 4 (over x, core).
Axes of the slice: x: 2, y: 2, z: 4, core: 2. Of those that a mesh axis runs over, the one named last changes fastest.
Arguments:
- query: bfloat16 [16, 7168], P(('group', 'seq'), 'tensor'), parts along dimension 0, may hold values from -5 to 5
- key_cache: bfloat16 [32, 256, 7168], P(('group', 'seq'), None, 'tensor'), parts along dimension 0, may hold values from -5 to 5
- value_cache: bfloat16 [32, 256, 7168], P(('group', 'seq'), None, 'tensor'), parts along dimension 0, may hold values from -6 to 6
- alibi_slopes: float32 [56], P('tensor'), may hold values from 0 to 1, as said below
- block_seq: int32 [32], P(('group', 'seq')), parts along dimension 0, may hold values from 0 to 7, as said below
- block_pos: int32 [32], P(('group', 'seq')), parts along dimension 0, may hold values from 0 to 2, as said below
- lengths: int32 [16], P('group'), parts along dimension 0, may hold values from 1 to 768, as said below
- out_weight: bfloat16 [7168, 14336], P('tensor', 'seq'), may hold values from -0.5 to 0.5
Outputs:
- mixed: bfloat16 [16, 14336], P(('group', 'tensor'), 'seq'), parts along dimension 0
There are 2 independent parts, one for each index of `group`. A program takes and returns all parts, laid end to end along the dimension named above; an argument that names none is the same for every part. Nothing has to cross between parts.
Inputs may be any that keep to these rules, and one draw needn't show every extreme that they name: `block_seq`: every sequence owns at least one block and at most 3; the blocks of sequence s have block_pos 0 to n_s - 1, each once. block_pos of a block is below the number of blocks its sequence owns. `lengths`: A sequence that owns n blocks has a length above 256 * (n - 1) and at most 256 * n. `alibi_slopes`: positive slopes.
All inputs are finite; a program needn't handle non-finite values.
Results may differ from a plain program's by a relative error of at most 0.0054.
Values may be sent and summed in bfloat16 or wider, within the bound.
No kernel may reach another device: no remote copies, remote signals or barrier semaphores. Data moves between devices by JAX's collectives and lax.ppermute only.
A program may use at most 64 MiB of HBM per device.

v0:
```python
import math

import jax
import jax.numpy as jnp
from jax import lax
from jax.sharding import PartitionSpec as P


def local(query, key_cache, value_cache, alibi_slopes, block_seq, block_pos, lengths, out_weight):
    heads = alibi_slopes.shape[0]
    features = query.shape[1]
    head_size = features // heads
    blocks_here = key_cache.shape[0]
    block_len = key_cache.shape[1]
    seq_count = lengths.shape[0]
    scale = 1.0 / math.sqrt(head_size)
    whole_query = lax.all_gather(query, "seq", axis=0, tiled=True)
    query_rows = jnp.take(whole_query, block_seq, axis=0).reshape(blocks_here, heads, head_size)
    keys = key_cache.reshape(blocks_here, block_len, heads, head_size)
    values = value_cache.reshape(blocks_here, block_len, heads, head_size)
    scores = (
        jnp.einsum("bthd,bhd->bht", keys, query_rows, preferred_element_type=jnp.float32) * scale
    )
    owner_length = lengths[block_seq]
    placed = block_pos[:, None] * block_len + jnp.arange(block_len, dtype=jnp.int32)[None, :]
    live = (placed < owner_length[:, None])[:, None, :]
    distance = (owner_length[:, None] - 1 - placed).astype(jnp.float32)
    scores = scores - alibi_slopes[None, :, None] * distance[:, None, :]
    scores = jnp.where(live, scores, -1e30)
    block_top = jnp.max(scores, axis=2)
    weights = jnp.where(live, jnp.exp(scores - block_top[:, :, None]), 0.0)
    block_total = jnp.sum(weights, axis=2)
    block_acc = jnp.einsum(
        "bht,bthd->bhd", weights.astype(jnp.bfloat16), values, preferred_element_type=jnp.float32
    )
    seq_ids = jnp.arange(seq_count, dtype=jnp.int32)
    owned = (block_seq[None, :] == seq_ids[:, None])[:, :, None]
    local_top = jnp.max(jnp.where(owned, block_top[None], -1e30), axis=1)
    factor = jnp.where(owned, jnp.exp(block_top[None] - local_top[:, None, :]), 0.0)
    local_total = jnp.sum(factor * block_total[None], axis=1)
    local_acc = jnp.einsum("sbh,bhd->shd", factor, block_acc, precision=lax.Precision.HIGHEST)
    tops, totals, accs = (
        lax.all_to_all(local_top[None], "seq", split_axis=1, concat_axis=0, tiled=True),
        lax.all_to_all(local_total[None], "seq", split_axis=1, concat_axis=0, tiled=True),
        lax.all_to_all(local_acc[None], "seq", split_axis=1, concat_axis=0, tiled=True),
    )
    best = jnp.max(tops, axis=0)
    scaling = jnp.exp(tops - best[None])
    home_total = jnp.sum(totals * scaling, axis=0)
    home_acc = jnp.sum(accs * scaling[..., None], axis=0)
    mine = (
        (home_acc / home_total[:, :, None])
        .astype(jnp.bfloat16)
        .reshape(home_acc.shape[0], features)
    )
    attention = lax.all_gather(mine, "seq", axis=0, tiled=True)
    mixed = lax.psum_scatter(
        jnp.dot(attention, out_weight, preferred_element_type=jnp.float32),
        "tensor",
        scatter_dimension=0,
        tiled=True,
    )
    return mixed.astype(jnp.bfloat16)


def solution(mesh):
    placed = (
        P(("group", "seq"), "tensor"),
        P(("group", "seq"), None, "tensor"),
        P(("group", "seq"), None, "tensor"),
        P("tensor"),
        P(("group", "seq")),
        P(("group", "seq")),
        P("group"),
        P("tensor", "seq"),
    )
    return jax.shard_map(
        local, mesh=mesh, in_specs=placed, out_specs=P(("group", "tensor"), "seq"), check_vma=False
    )
```

profile of v0, /device:TPU:0, one launch (start us, length us, event | category | flops | bytes accessed | tf_op | source)
XLA Modules:
  0.0 95.4 jit_solution(14486349411866468453)
XLA Ops:
  0.0 0.0 copy-start
  0.0 0.7 compare_select_fusion
  0.7 0.7 compare_and_fusion
  1.3 0.7 iota_compare_fusion
  2.1 0.0 copy-done
  2.1 0.6 gather_fusion
  2.7 0.7 broadcast_add_fusion
  3.4 0.1 fusion.16
  3.5 0.1 subtract_convert_fusion
  3.5 15.1 %all-gather = bf16[4,2,1792]{2,1,0:T(2,128)(2,1)S(1)} all-gather(bf16[1,2,1792]{2,1,0:T(2,128)(2,1)} %bitcast.41), channel_id=1, replica_groups=mesh['group'=2,'seq'=4,'tensor'=4] {'seq'}, dimensions={0}, use_global_device_ids=true | all-gather | bytes 35840 | tf_op jit(solution)/shard_map/all_gather | solution.py:17
  18.6 0.6 gather_fusion.1
  19.2 6.0 %copy.49 = bf16[4,256,1792]{1,2,0:T(8,128)(2,1)} copy(bf16[4,256,1792]{2,1,0:T(8,128)(2,1)} %param.9) | data formatting | bytes 7340032 | tf_op args[1]
  25.2 0.0 copy-start.1
  25.2 0.1 select_bitcast_fusion
  25.3 2.6 %fusion.9 = f32[4,14,1,256]{3,2,1,0:T(1,128)S(1)} fusion(bf16[4,256,14,128]{1,3,2,0:T(8,128)(2,1)} %bitcast.33, bf16[4,14,128,1]{2,1,0,3:T(8,128)(2,1)S(1)} %select_bitcast_fusion), kind=kOutput, calls=%fused_computation.16 | convolution fusion | flops 3670016 | bytes 3741696 | tf_op jit(solution)/shard_map/bthd,bhd->bht/dot_general | solution.py:22
  27.9 0.0 copy-done.1
  27.9 0.2 fusion.18
  28.0 0.1 select_reduce_fusion
  28.1 0.7 copy.54
  28.8 4.7 %all-to-all-start.1 = ((f32[1,8,14]{2,0,1:T(1,128)}), f32[1,8,14]{2,0,1:T(1,128)S(1)}, u32[]{:S(2)}, u32[]{:S(2)}) async-start(f32[1,8,14]{2,0,1:T(1,128)} %copy.54), calls=%async_computation.1 | async-start | bytes 8192 | tf_op jit(solution)/shard_map/all_to_all | solution.py:43
  33.6 0.2 fusion.4
  33.7 0.1 multiply_reduce_fusion.1
  33.8 6.0 %copy.50 = bf16[4,256,1792]{1,2,0:T(8,128)(2,1)} copy(bf16[4,256,1792]{2,1,0:T(8,128)(2,1)} %param.10) | data formatting | bytes 7340032 | tf_op args[2]
  39.8 0.0 copy-start.2
  39.8 3.1 %fusion.2 = f32[4,14,1,128]{3,2,1,0:T(1,128)S(1)} fusion(bf16[4,256,14,128]{1,3,2,0:T(8,128)(2,1)} %bitcast.34, bf16[4,14,256,1]{2,0,1,3:T(4,128)(2,1)S(1)} %get-tuple-element.10), kind=kOutput, calls=%fused_computation.6 | convolution fusion | flops 3670016 | bytes 3727360 | tf_op jit(solution)/shard_map/bht,bthd->bhd/dot_general | solution.py:33
  42.9 0.4 convolution_bitcast_fusion
  43.3 0.7 copy.57
  44.0 0.0 all-to-all-done.1
  44.0 5.1 %all-to-all-start.2 = ((f32[1,8,14]{2,0,1:T(1,128)}), f32[1,8,14]{2,0,1:T(1,128)S(1)}, u32[]{:S(2)}, u32[]{:S(2)}) async-start(f32[1,8,14]{2,0,1:T(1,128)} %copy.57), calls=%async_computation.2 | async-start | bytes 8192 | tf_op jit(solution)/shard_map/all_to_all | solution.py:44
  49.1 0.7 copy.51
  49.7 0.0 copy-done.2
  49.7 0.6 dynamic-slice
  51.0 3.7 %all-to-all-done.2 = f32[1,8,14]{2,0,1:T(1,128)S(1)} async-done(((f32[1,8,14]{2,0,1:T(1,128)}), f32[1,8,14]{2,0,1:T(1,128)S(1)}, u32[]{:S(2)}, u32[]{:S(2)}) %all-to-all-start.2) | async-done | bytes 480 | tf_op jit(solution)/shard_map/all_to_all | solution.py:44
  54.6 3.3 %all-to-all-start = ((f32[1,8,14,128]{3,0,2,1:T(1,128)}), f32[1,8,14,128]{3,0,2,1:T(1,128)S(1)}, u32[]{:S(2)}, u32[]{:S(2)}) async-start(f32[1,8,14,128]{3,0,2,1:T(1,128)} %copy.51), calls=%async_computation | async-start | bytes 114688 | tf_op jit(solution)/shard_map/all_to_all | solution.py:45
  58.0 0.1 copy.55
  58.1 0.1 copy.58
  58.2 5.5 %all-to-all-done = f32[1,8,14,128]{3,0,2,1:T(1,128)S(1)} async-done(((f32[1,8,14,128]{3,0,2,1:T(1,128)}), f32[1,8,14,128]{3,0,2,1:T(1,128)S(1)}, u32[]{:S(2)}, u32[]{:S(2)}) %all-to-all-start) | async-done | bytes 57376 | tf_op jit(solution)/shard_map/all_to_all | solution.py:45
  63.6 0.1 multiply_reduce_fusion
  63.8 0.1 fusion.15
  63.9 13.2 %all-gather.1 = bf16[4,2,1792]{2,1,0:T(2,128)(2,1)S(1)} all-gather(bf16[1,2,1792]{2,1,0:T(2,128)(2,1)S(1)} %fusion.15), channel_id=1, replica_groups=mesh['group'=2,'seq'=4,'tensor'=4] {'seq'}, dimensions={0}, use_global_device_ids=true | all-gather | bytes 35840 | tf_op jit(solution)/shard_map/all_gather | solution.py:56
  77.1 6.4 %fusion.20 = f32[8,3584]{1,0:T(8,128)S(1)} fusion(bf16[8,1792]{1,0:T(8,128)(2,1)S(1)} %reshape.152, bf16[1792,3584]{1,0:T(8,128)(2,1)} %param.15), kind=kOutput, calls=%fused_computation.41 | convolution fusion | flops 102760448 | bytes 12988416 | tf_op jit(solution)/shard_map/dot_general | solution.py:58
  83.5 11.3 %all-reduce = bf16[8,3584]{1,0:T(8,128)(2,1)S(1)} all-reduce(f32[8,3584]{1,0:T(8,128)S(1)} %fusion.20), channel_id=2, replica_groups=mesh['group'=2,'seq'=4,'tensor'=4] {'tensor'}, use_global_device_ids=true, to_apply=%region_7.8.clone | all-reduce | flops 28672 | bytes 172032
  94.7 0.6 dynamic-slice_convert_fusion
  (7 shorter events, 0.1 us)
Async XLA Ops:
  0.0 2.1 %copy-start = (s32[8]{0:T(128)S(1)}, s32[8]{0:T(128)}, u32[]{:S(2)}) copy-start(s32[8]{0:T(128)} %param.14) | copy-start | bytes 100
  25.2 2.7 %copy-start.1 = (f32[14]{0:T(128)S(1)}, f32[14]{0:T(128)}, u32[]{:S(2)}) copy-start(f32[14]{0:T(128)} %param.11) | copy-start | bytes 172
  28.8 15.2 %all-to-all-start.1 = ((f32[1,8,14]{2,0,1:T(1,128)}), f32[1,8,14]{2,0,1:T(1,128)S(1)}, u32[]{:S(2)}, u32[]{:S(2)}) async-start(f32[1,8,14]{2,0,1:T(1,128)} %copy.54), calls=%async_computation.1 | async-start | bytes 8192 | tf_op jit(solution)/shard_map/all_to_all | solution.py:43
  39.8 9.9 %copy-start.2 = (u32[32]{0:T(128)S(1)}, u32[32]{0:T(128)}, u32[]{:S(2)}) copy-start(u32[32]{0:T(128)} %constant.39) | copy-start | bytes 388
  44.0 10.7 %all-to-all-start.2 = ((f32[1,8,14]{2,0,1:T(1,128)}), f32[1,8,14]{2,0,1:T(1,128)S(1)}, u32[]{:S(2)}, u32[]{:S(2)}) async-start(f32[1,8,14]{2,0,1:T(1,128)} %copy.57), calls=%async_computation.2 | async-start | bytes 8192 | tf_op jit(solution)/shard_map/all_to_all | solution.py:44
  54.6 9.0 %all-to-all-start = ((f32[1,8,14,128]{3,0,2,1:T(1,128)}), f32[1,8,14,128]{3,0,2,1:T(1,128)S(1)}, u32[]{:S(2)}, u32[]{:S(2)}) async-start(f32[1,8,14,128]{3,0,2,1:T(1,128)} %copy.51), calls=%async_computation | async-start | bytes 114688 | tf_op jit(solution)/shard_map/all_to_all | solution.py:45
where the time goes:
time: 96.1 us; the launch traced here: 95.4 us
  blocking collectives  39.5 us (41%)
  local copies, waits for them, and re-layouts  16.7 us (17%)
  starting transfers between devices  13.1 us (14%)
  matrix products  12.5 us (13%)
  waiting for transfers between devices  9.12 us (9%)
  other arithmetic  3.75 us (4%)
    all_gather x1, blocking collectives, local(): whole_query = lax.all_gather(query, 'seq', axis=0, tiled=True)  15.1 us
    all_gather x1, blocking collectives, local(): attention = lax.all_gather(mine, 'seq', axis=0, tiled=True)  13.2 us
    unnamed x11, local copies, waits for them, and re-layouts  12.6 us
    unnamed x1, blocking collectives  11.3 us
    dot_general x1, matrix products, local(): jnp.dot(attention, out_weight, preferred_element_type=jnp.float32)  6.41 us
    all_to_all x1, waiting for transfers between devices, local(): lax.all_to_all(local_acc[None], 'seq', split_axis=1, concat_axis=0, tiled...  5.46 us
    all_to_all x1, starting transfers between devices, local(): lax.all_to_all(local_total[None], 'seq', split_axis=1, concat_axis=0, til...  5.09 us
    all_to_all x1, starting transfers between devices, local(): lax.all_to_all(local_top[None], 'seq', split_axis=1, concat_axis=0, tiled...  4.74 us
  transfers between devices with their start and end apart: 3, of which 2 were waited for; matrix products, arithmetic and copies ran while one was open for 13% of the time, Pallas kernels for 0%

commit v1 on v0

v1 whole, which is shorter than its diff:
```python
import math
from functools import partial

import jax
import jax.numpy as jnp
from jax import lax
from jax.experimental import pallas as pl
from jax.experimental.pallas import tpu as pltpu
from jax.sharding import PartitionSpec as P

F32 = jnp.float32
BF16 = jnp.bfloat16
LANES = 128
DEAD = -1e30
DIRECT = 8
VMEM = pl.BlockSpec(memory_space=pltpu.VMEM)
SMEM = pl.BlockSpec(memory_space=pltpu.SMEM)


def params(mib):
    return pltpu.CompilerParams(vmem_limit_bytes=mib << 20)


def from_peers(x, axis):
    size = lax.axis_size(axis)
    if size > DIRECT or size & (size - 1):
        return [lax.all_gather(x, axis, axis=0, tiled=True)]
    return [x] + [swap(x, axis, m) for m in range(1, size)]


def swap(x, axis, m):
    size = lax.axis_size(axis)
    return lax.ppermute(x, axis, [(i, i ^ m) for i in range(size)])


def pad_rows(n):
    return -(-n // 16) * 16


def prep_kernel(slopes, block_seq, block_pos, lengths, bias, pick, owner, *, direct):
    blocks, rows, block_len = bias.shape
    seqs = pick.shape[1]
    here = lax.axis_index("seq") if direct else 0
    per_home = seqs // lax.axis_size("seq")
    head = lax.broadcasted_iota(jnp.int32, (rows, block_len), 0)
    slope = jnp.zeros((rows, block_len), F32)
    for h in range(slopes.shape[0]):
        slope = jnp.where(head == h, slopes[h], slope)
    offset = lax.broadcasted_iota(jnp.int32, (rows, block_len), 1)
    row = lax.broadcasted_iota(jnp.int32, (seqs, LANES), 0)
    for b in range(blocks):
        seq = block_seq[b]
        length = lengths[seq]
        place = block_pos[b] * block_len + offset
        distance = (length - 1 - place).astype(F32)
        bias[b] = jnp.where(place < length, -(slope * distance), DEAD)
        at = ((seq // per_home) ^ here) * per_home + seq % per_home
        pick[b] = jnp.where(row == at, 1.0, 0.0).astype(F32)
        owner[b : b + 1, :] = jnp.full((1, LANES), seq, jnp.int32).astype(F32)


def attend_kernel(bias, pick, owner, keys, values, *rest, scale, heads):
    queries, out, whole = rest[:-2], rest[-2], rest[-1]
    blocks, rows, _ = bias.shape
    features = keys.shape[2]
    size = features // heads
    at = 0
    for part in queries:
        whole[at : at + part.shape[0], :] = part[...].astype(F32)
        at += part.shape[0]
    head = lax.broadcasted_iota(jnp.int32, (rows, size), 0)
    row = lax.broadcasted_iota(jnp.int32, (rows, LANES), 0)
    lane = lax.broadcasted_iota(jnp.int32, (rows, LANES), 1)
    all_rows = whole[...]
    for b in range(blocks):
        mine = pick[b]
        spread = []
        for h in range(heads):
            query = jnp.sum(all_rows[:, h * size : (h + 1) * size] * mine[:, :size], axis=0, keepdims=True)
            spread.append(jnp.where(head == h, query, 0.0))
        query = jnp.concatenate(spread, axis=1).astype(BF16)
        scores = lax.dot_general(query, keys[b], (((1,), (1,)), ((), ())), preferred_element_type=F32)
        scores = scores * scale + bias[b]
        top = jnp.max(scores, axis=1, keepdims=True)
        weights = jnp.exp(scores - top)
        total = jnp.sum(weights, axis=1, keepdims=True)
        sums = jnp.dot(weights.astype(BF16), values[b], preferred_element_type=F32)
        for h in range(heads):
            out[b : b + 1, h * size : (h + 1) * size] = sums[h : h + 1, h * size : (h + 1) * size]
        stats = jnp.where(lane == row, top, 0.0) + jnp.where(lane == row + LANES // 2, total, 0.0)
        out[b : b + 1, features : features + LANES] = jnp.sum(stats, axis=0, keepdims=True)
        out[b : b + 1, features + LANES :] = owner[b : b + 1, :]


def project_kernel(weight, *rest, heads, parts):
    partials, outs, acc = rest[:parts], rest[parts:-1], rest[-1]
    seqs = acc.shape[0]
    features = weight.shape[0]
    size = features // heads
    peers = len(outs)
    each = seqs // peers
    t = lax.axis_index("tensor")
    row = lax.broadcasted_iota(jnp.int32, (seqs, LANES), 0)
    target = (((row // each) ^ t) * each + row % each).astype(F32)

    def stats_of(line):
        mine = line[:, features + LANES :] == target
        stats = jnp.broadcast_to(line[:, features : features + LANES], (seqs, LANES))
        return mine, stats

    def over_blocks(step, carry):
        for ref in partials:
            count = ref.shape[0]
            if count <= 8 or count % 8:
                for b in range(count):
                    carry = step(ref[b : b + 1, :], carry)
            else:

                def eight(g, carry, ref=ref):
                    lines = ref[pl.ds(pl.multiple_of(g * 8, 8), 8), :]
                    for b in range(8):
                        carry = step(lines[b : b + 1], carry)
                    return carry

                carry = lax.fori_loop(0, count // 8, eight, carry)
        return carry

    def highest(line, best):
        mine, stats = stats_of(line)
        return jnp.maximum(best, jnp.where(mine, stats, DEAD))

    best = over_blocks(highest, jnp.full((seqs, LANES), DEAD, F32))

    def add_up(line, carry):
        total, sums = carry
        mine, stats = stats_of(line)
        factor = jnp.where(mine, jnp.exp(stats - best), 0.0)
        total = total + factor * pltpu.roll(stats, LANES // 2, 1)
        new = []
        for h in range(heads):
            value = line[:, h * size : (h + 1) * size]
            new.append(sums[h] + jnp.broadcast_to(factor[:, h : h + 1], (seqs, size)) * value)
        return total, tuple(new)

    zeros = tuple(jnp.zeros((seqs, size), F32) for _ in range(heads))
    total, sums = over_blocks(add_up, (jnp.zeros((seqs, LANES), F32), zeros))
    for h in range(heads):
        acc[:, h * size : (h + 1) * size] = sums[h] / total[:, h : h + 1]
    attention = acc[...].astype(BF16)
    columns = weight.shape[1]
    step = 512 if columns % 512 == 0 else columns
    for c in range(0, columns, step):
        mixed = jnp.dot(attention, weight[:, c : c + step], preferred_element_type=F32)
        for m, out in enumerate(outs):
            out[:, c : c + step] = mixed[m * each : (m + 1) * each]


def local(query, key_cache, value_cache, alibi_slopes, block_seq, block_pos, lengths, out_weight):
    heads = alibi_slopes.shape[0]
    features = query.shape[1]
    blocks, block_len = key_cache.shape[:2]
    seqs = lengths.shape[0]
    columns = out_weight.shape[1]
    peers = lax.axis_size("tensor")
    rows = pad_rows(heads)
    scale = 1.0 / math.sqrt(features // heads)
    keys, values, weight = (
        pltpu.with_memory_space_constraint(a, pltpu.VMEM) for a in (key_cache, value_cache, out_weight)
    )
    queries = from_peers(query, "seq")
    bias, pick, owner = pl.pallas_call(
        partial(prep_kernel, direct=len(queries) > 1),
        out_shape=[
            jax.ShapeDtypeStruct((blocks, rows, block_len), F32),
            jax.ShapeDtypeStruct((blocks, seqs, LANES), F32),
            jax.ShapeDtypeStruct((blocks, LANES), F32),
        ],
        in_specs=[SMEM] * 4,
        out_specs=[VMEM] * 3,
        compiler_params=params(4),
        cost_estimate=pl.CostEstimate(flops=20_000_000_000, transcendentals=0, bytes_accessed=1 << 16),
        name="prep",
    )(alibi_slopes, block_seq, block_pos, lengths)
    partial_rows = pl.pallas_call(
        partial(attend_kernel, scale=scale, heads=heads),
        out_shape=jax.ShapeDtypeStruct((blocks, features + 2 * LANES), F32),
        in_specs=[VMEM] * (5 + len(queries)),
        out_specs=VMEM,
        scratch_shapes=[pltpu.VMEM((seqs, features), F32)],
        compiler_params=params(12),
        name="attend",
    )(bias, pick, owner, keys, values, *queries)
    partials = from_peers(partial_rows, "seq")
    mixed = pl.pallas_call(
        partial(project_kernel, heads=heads, parts=len(partials)),
        out_shape=[jax.ShapeDtypeStruct((seqs // peers, columns), F32)] * peers,
        in_specs=[VMEM] * (1 + len(partials)),
        out_specs=[VMEM] * peers,
        scratch_shapes=[pltpu.VMEM((seqs, features), F32)],
        compiler_params=params(12),
        name="project",
    )(weight, *partials)
    whole = mixed[0]
    for m in range(1, peers):
        whole = whole + swap(mixed[m], "tensor", m)
    return whole.astype(BF16)


def solution(mesh):
    placed = (
        P(("group", "seq"), "tensor"),
        P(("group", "seq"), None, "tensor"),
        P(("group", "seq"), None, "tensor"),
        P("tensor"),
        P(("group", "seq")),
        P(("group", "seq")),
        P("group"),
        P("tensor", "seq"),
    )
    return jax.shard_map(
        local, mesh=mesh, in_specs=placed, out_specs=P(("group", "tensor"), "seq"), check_vma=False
    )
```

time: 96.1 us -> 29.3 us (0.30)
  blocking collectives: 39.5 us -> 0 us
  local copies, waits for them, and re-layouts: 16.7 us -> 2.63 us
  matrix products: 12.5 us -> 0 us
  Pallas kernels: 0 us -> 6.18 us
  other arithmetic: 3.75 us -> 0.63 us
  waiting for transfers between devices: 9.12 us -> 7.6 us
  starting transfers between devices: 13.1 us -> 12 us
    all_gather x2 -> x0, blocking collectives: 28.2 us -> none  [the longest x1 15.1 us: local(): whole_query = lax.all_gather(query, 'seq', axis=0, tiled=True)]
    all_to_all x3 -> x0, starting transfers between devices: 13.1 us -> none  [the longest x1 5.09 us: local(): lax.all_to_all(local_total[None], 'seq', split_axis=1, concat_axis=0, til...]
    dot_general x4 -> x0, matrix products: 12.5 us -> none  [the longest x1 6.41 us: local(): jnp.dot(attention, out_weight, preferred_element_type=jnp.float32)]
    ppermute x0 -> x9, starting transfers between devices: none -> 12 us  [swap(): return lax.ppermute(x, axis, [(i, i ^ m) for i in range(size)])]
    unnamed x1 -> x0, blocking collectives: 11.3 us -> none
    unnamed x11 -> x16, local copies, waits for them, and re-layouts: 12.6 us -> 2.63 us
    all_to_all x3 -> x0, waiting for transfers between devices: 9.12 us -> none  [the longest x1 5.46 us: local(): lax.all_to_all(local_acc[None], 'seq', split_axis=1, concat_axis=0, tiled...]
    ppermute x0 -> x9, waiting for transfers between devices: none -> 7.6 us  [swap(): return lax.ppermute(x, axis, [(i, i ^ m) for i in range(size)])]
  transfers between devices with their start and end apart: 3 -> 9, of which waited for: 2 -> 6; matrix products, arithmetic and copies ran while one was open for 13% -> 0% of each run, Pallas kernels for 0% -> 2%
where the time goes in v1:
time: 29.3 us; the launch traced here: 29.1 us
  starting transfers between devices  12 us (41%)
  waiting for transfers between devices  7.6 us (26%)
  Pallas kernels  6.18 us (21%)
  local copies, waits for them, and re-layouts  2.63 us (9%)
  other arithmetic  0.63 us (2%)
    ppermute x9, starting transfers between devices, swap(): return lax.ppermute(x, axis, [(i, i ^ m) for i in range(size)])  12 us
    ppermute x9, waiting for transfers between devices, swap(): return lax.ppermute(x, axis, [(i, i ^ m) for i in range(size)])  7.6 us
    pallas_call x1, Pallas kernels, local(): pl.pallas_call(partial(attend_kernel, scale=scale, heads=heads), out_shap...  3.59 us
    unnamed x16, local copies, waits for them, and re-layouts  2.63 us
    pallas_call x1, Pallas kernels, local(): pl.pallas_call(partial(project_kernel, heads=heads, parts=len(partials)),...  1.99 us
    convert_element_type x1, other arithmetic, local(): return whole.astype(BF16)  0.63 us
    pallas_call x1, Pallas kernels, local(): pl.pallas_call(partial(prep_kernel, direct=len(queries) > 1), out_shape=[...  0.6 us
  transfers between devices with their start and end apart: 9, of which 6 were waited for; matrix products, arithmetic and copies ran while one was open for 0% of the time, Pallas kernels for 2%

profile of v1, /device:TPU:0, one launch (start us, length us, event | category | flops | bytes accessed | tf_op | source)
XLA Modules:
  0.0 29.1 jit_solution(5224966455531742994)
XLA Ops:
  0.0 0.0 copy-start.3
  0.0 0.0 copy-start.2
  0.0 0.0 copy-start.1
  0.0 4.1 %collective-permute-start.1 = (bf16[2,1792]{1,0:T(2,128)(2,1)}, bf16[2,1792]{1,0:T(2,128)(2,1)S(1)}, u32[]{:S(2)}, u32[]{:S(2)}) collective-permute-start(bf16[2,1792]{1,0:T(2,128)(2,1)} %rest_0_.1), channel_id=1, source_target_pairs={{0,8},{4,12},{8,0},{12,4},{1,9},{5,13},{9,1},{13,5},{2,10},{6,14},... | collective-permute-start | bytes 21512 | tf_op jit(solution)/shard_map/ppermute | solution.py:33
  4.1 1.6 %collective-permute-start = (bf16[2,1792]{1,0:T(2,128)(2,1)}, bf16[2,1792]{1,0:T(2,128)(2,1)S(1)}, u32[]{:S(2)}, u32[]{:S(2)}) collective-permute-start(bf16[2,1792]{1,0:T(2,128)(2,1)} %rest_0_.1), channel_id=1, source_target_pairs={{0,4},{4,0},{8,12},{12,8},{1,5},{5,1},{9,13},{13,9},{2,6},{6,2},{1... | collective-permute-start | bytes 21512 | tf_op jit(solution)/shard_map/ppermute | solution.py:33
  5.7 0.0 collective-permute-start.2
  5.7 0.0 copy-start.4
  5.7 0.7 %copy-done.4 = f32[14]{0:T(128)S(1)} copy-done((f32[14]{0:T(128)S(1)}, f32[14]{0:T(128)}, u32[]{:S(2)}) %copy-start.4) | copy-done | bytes 80
  6.4 0.0 copy-start.5
  6.4 0.7 %copy-done.5 = s32[4]{0:T(128)S(1)} copy-done((s32[4]{0:T(128)S(1)}, s32[4]{0:T(128)}, u32[]{:S(2)}) %copy-start.5) | copy-done | bytes 40
  7.0 0.0 copy-start.6
  7.0 0.7 %copy-done.6 = s32[4]{0:T(128)S(1)} copy-done((s32[4]{0:T(128)S(1)}, s32[4]{0:T(128)}, u32[]{:S(2)}) %copy-start.6) | copy-done | bytes 40
  7.7 0.0 copy-start.7
  7.7 0.7 %copy-done.7 = s32[8]{0:T(128)S(1)} copy-done((s32[8]{0:T(128)S(1)}, s32[8]{0:T(128)}, u32[]{:S(2)}) %copy-start.7) | copy-done | bytes 56
  8.3 0.0 copy-start
  8.3 0.6 %prep.1 = (f32[4,16,256]{2,1,0:T(8,128)S(1)}, f32[4,8,128]{2,1,0:T(8,128)S(1)}, f32[4,128]{1,0:T(4,128)S(1)}) custom-call(f32[14]{0:T(128)S(1)} %copy-done.4, s32[4]{0:T(128)S(1)} %copy-done.5, s32[4]{0:T(128)S(1)} %copy-done.6, s32[8]{0:T(128)S(1)} %copy-done.7), custom_call_target="tpu_custom_call" | custom-call | flops 20000000000 | bytes 65536 | tf_op jit(solution)/shard_map/prep/pallas_call | solution.py:171
  9.0 0.0 collective-permute-done.1.rest_2_
  9.0 0.0 collective-permute-done.rest_1_
  9.0 2.4 %collective-permute-done.2.rest_3_ = bf16[2,1792]{1,0:T(2,128)(2,1)S(1)} collective-permute-done((bf16[2,1792]{1,0:T(2,128)(2,1)}, bf16[2,1792]{1,0:T(2,128)(2,1)S(1)}, u32[]{:S(2)}, u32[]{:S(2)}) %collective-permute-start.2) | collective-permute-done | bytes 7200 | tf_op jit(solution)/shard_map/ppermute | solution.py:33
  11.4 0.0 copy-done.3
  11.4 0.0 copy-done.2
  11.4 0.0 copy-done.1
  11.4 3.6 %attend.1.rest_0_ = f32[4,2048]{1,0:T(4,128)S(1)} custom-call(f32[4,16,256]{2,1,0:T(8,128)S(1)} %get-tuple-element.12.bias, f32[4,8,128]{2,1,0:T(8,128)S(1)} %get-tuple-element.13.pick, f32[4,128]{1,0:T(4,128)S(1)} %get-tuple-element.14.owner, bf16[4,256,1792]{2,1,0:T(8,128)(2,1)S(1)} %copy-done.1, bf16[4,256,1792]{2,1,0:T(8,128)(2,1)S(1)} %copy-done.2, ...), custom_call_target="tpu_custom_call" | custom-call | tf_op jit(solution)/shard_map/attend/pallas_call | solution.py:184
  15.0 1.5 %collective-permute-start.5 = (f32[4,2048]{1,0:T(4,128)S(1)}, f32[4,2048]{1,0:T(4,128)S(1)}, u32[]{:S(2)}, u32[]{:S(2)}) collective-permute-start(f32[4,2048]{1,0:T(4,128)S(1)} %attend.1.rest_0_), channel_id=1, source_target_pairs={{0,12},{4,8},{8,4},{12,0},{1,13},{5,9},{9,5},{13,1},{2,14},{6,10},... | collective-permute-start | bytes 98312 | tf_op jit(solution)/shard_map/ppermute | solution.py:33
  16.5 0.0 collective-permute-start.4
  16.5 2.9 %collective-permute-start.3 = (f32[4,2048]{1,0:T(4,128)S(1)}, f32[4,2048]{1,0:T(4,128)S(1)}, u32[]{:S(2)}, u32[]{:S(2)}) collective-permute-start(f32[4,2048]{1,0:T(4,128)S(1)} %attend.1.rest_0_), channel_id=1, source_target_pairs={{0,4},{4,0},{8,12},{12,8},{1,5},{5,1},{9,13},{13,9},{2,6},{6,2},{1... | collective-permute-start | bytes 98312 | tf_op jit(solution)/shard_map/ppermute | solution.py:33
  19.4 1.3 %collective-permute-done.5.rest_3_ = f32[4,2048]{1,0:T(4,128)S(1)} collective-permute-done((f32[4,2048]{1,0:T(4,128)S(1)}, f32[4,2048]{1,0:T(4,128)S(1)}, u32[]{:S(2)}, u32[]{:S(2)}) %collective-permute-start.5) | collective-permute-done | bytes 32800 | tf_op jit(solution)/shard_map/ppermute | solution.py:33
  20.8 0.8 %collective-permute-done.4.rest_2_ = f32[4,2048]{1,0:T(4,128)S(1)} collective-permute-done((f32[4,2048]{1,0:T(4,128)S(1)}, f32[4,2048]{1,0:T(4,128)S(1)}, u32[]{:S(2)}, u32[]{:S(2)}) %collective-permute-start.4) | collective-permute-done | bytes 32800 | tf_op jit(solution)/shard_map/ppermute | solution.py:33
  21.6 0.1 collective-permute-done.3.rest_1_
  21.7 0.0 copy-done
  21.7 2.0 %project.1 = (f32[2,3584]{1,0:T(2,128)S(1)}, f32[2,3584]{1,0:T(2,128)S(1)}, f32[2,3584]{1,0:T(2,128)S(1)}, f32[2,3584]{1,0:T(2,128)S(1)}) custom-call(bf16[1792,3584]{1,0:T(8,128)(2,1)S(1)} %copy-done, f32[4,2048]{1,0:T(4,128)S(1)} %attend.1.rest_0_, f32[4,2048]{1,0:T(4,128)S(1)} %collective-permute-done.3.rest_1_, ...), custom_call_target="tpu_custom_call" | custom-call | tf_op jit(solution)/shard_map/project/pallas_call | solution.py:194
  23.7 0.0 collective-permute-start.6
  23.7 1.5 %collective-permute-start.7 = (f32[2,3584]{1,0:T(2,128)S(1)}, f32[2,3584]{1,0:T(2,128)S(1)}, u32[]{:S(2)}, u32[]{:S(2)}) collective-permute-start(f32[2,3584]{1,0:T(2,128)S(1)} %get-tuple-element.17), channel_id=1, source_target_pairs={{0,2},{1,3},{2,0},{3,1},{4,6},{5,7},{6,4},{7,5},{8,10},{9,11},{10,... | collective-permute-start | bytes 86024 | tf_op jit(solution)/shard_map/ppermute | solution.py:33
  25.2 0.3 %collective-permute-start.8 = (f32[2,3584]{1,0:T(2,128)S(1)}, f32[2,3584]{1,0:T(2,128)S(1)}, u32[]{:S(2)}, u32[]{:S(2)}) collective-permute-start(f32[2,3584]{1,0:T(2,128)S(1)} %get-tuple-element.18), channel_id=1, source_target_pairs={{0,3},{1,2},{2,1},{3,0},{4,7},{5,6},{6,5},{7,4},{8,11},{9,10},{10,... | collective-permute-start | bytes 86024 | tf_op jit(solution)/shard_map/ppermute | solution.py:33
  25.5 0.0 collective-permute-done.6
  25.5 2.0 %collective-permute-done.7 = f32[2,3584]{1,0:T(2,128)S(1)} collective-permute-done((f32[2,3584]{1,0:T(2,128)S(1)}, f32[2,3584]{1,0:T(2,128)S(1)}, u32[]{:S(2)}, u32[]{:S(2)}) %collective-permute-start.7) | collective-permute-done | bytes 28704 | tf_op jit(solution)/shard_map/ppermute | solution.py:33
  27.6 0.9 %collective-permute-done.8 = f32[2,3584]{1,0:T(2,128)S(1)} collective-permute-done((f32[2,3584]{1,0:T(2,128)S(1)}, f32[2,3584]{1,0:T(2,128)S(1)}, u32[]{:S(2)}, u32[]{:S(2)}) %collective-permute-start.8) | collective-permute-done | bytes 28704 | tf_op jit(solution)/shard_map/ppermute | solution.py:33
  28.5 0.6 %add_convert_fusion = bf16[2,3584]{1,0:T(2,128)(2,1)} fusion(f32[2,3584]{1,0:T(2,128)S(1)} %collective-permute-done.8, f32[2,3584]{1,0:T(2,128)S(1)} %collective-permute-done.7, f32[2,3584]{1,0:T(2,128)S(1)} %get-tuple-element.15, f32[2,3584]{1,0:T(2,128)S(1)} %collective-permute-done.6), kind=kLoop, calls=%fused_computation | loop fusion | flops 28672 | bytes 129024 | tf_op jit(solution)/shard_map/convert_element_type | solution.py:206
Async XLA Ops:
  0.0 11.4 %copy-start.3 = (bf16[2,1792]{1,0:T(2,128)(2,1)S(1)}, bf16[2,1792]{1,0:T(2,128)(2,1)}, u32[]{:S(2)}) copy-start(bf16[2,1792]{1,0:T(2,128)(2,1)} %rest_0_.1) | copy-start | bytes 21508
  0.0 11.4 %copy-start.2 = (bf16[4,256,1792]{2,1,0:T(8,128)(2,1)S(1)}, bf16[4,256,1792]{2,1,0:T(8,128)(2,1)}, u32[]{:S(2)}) copy-start(bf16[4,256,1792]{2,1,0:T(8,128)(2,1)} %values.1) | copy-start | bytes 11010052
  0.0 11.4 %copy-start.1 = (bf16[4,256,1792]{2,1,0:T(8,128)(2,1)S(1)}, bf16[4,256,1792]{2,1,0:T(8,128)(2,1)}, u32[]{:S(2)}) copy-start(bf16[4,256,1792]{2,1,0:T(8,128)(2,1)} %keys.1) | copy-start | bytes 11010052
  0.0 9.0 %collective-permute-start.1 = (bf16[2,1792]{1,0:T(2,128)(2,1)}, bf16[2,1792]{1,0:T(2,128)(2,1)S(1)}, u32[]{:S(2)}, u32[]{:S(2)}) collective-permute-start(bf16[2,1792]{1,0:T(2,128)(2,1)} %rest_0_.1), channel_id=1, source_target_pairs={{0,8},{4,12},{8,0},{12,4},{1,9},{5,13},{9,1},{13,5},{2,10},{6,14},... | collective-permute-start | bytes 21512 | tf_op jit(solution)/shard_map/ppermute | solution.py:33
  4.1 4.8 %collective-permute-start = (bf16[2,1792]{1,0:T(2,128)(2,1)}, bf16[2,1792]{1,0:T(2,128)(2,1)S(1)}, u32[]{:S(2)}, u32[]{:S(2)}) collective-permute-start(bf16[2,1792]{1,0:T(2,128)(2,1)} %rest_0_.1), channel_id=1, source_target_pairs={{0,4},{4,0},{8,12},{12,8},{1,5},{5,1},{9,13},{13,9},{2,6},{6,2},{1... | collective-permute-start | bytes 21512 | tf_op jit(solution)/shard_map/ppermute | solution.py:33
  5.7 5.6 %collective-permute-start.2 = (bf16[2,1792]{1,0:T(2,128)(2,1)}, bf16[2,1792]{1,0:T(2,128)(2,1)S(1)}, u32[]{:S(2)}, u32[]{:S(2)}) collective-permute-start(bf16[2,1792]{1,0:T(2,128)(2,1)} %rest_0_.1), channel_id=1, source_target_pairs={{0,12},{4,8},{8,4},{12,0},{1,13},{5,9},{9,5},{13,1},{2,14},{6,10},... | collective-permute-start | bytes 21512 | tf_op jit(solution)/shard_map/ppermute | solution.py:33
  5.7 0.7 %copy-start.4 = (f32[14]{0:T(128)S(1)}, f32[14]{0:T(128)}, u32[]{:S(2)}) copy-start(f32[14]{0:T(128)} %slopes.1) | copy-start | bytes 172
  6.4 0.7 %copy-start.5 = (s32[4]{0:T(128)S(1)}, s32[4]{0:T(128)}, u32[]{:S(2)}) copy-start(s32[4]{0:T(128)} %block_seq.1) | copy-start | bytes 52
  7.0 0.7 %copy-start.6 = (s32[4]{0:T(128)S(1)}, s32[4]{0:T(128)}, u32[]{:S(2)}) copy-start(s32[4]{0:T(128)} %block_pos.1) | copy-start | bytes 52
  7.7 0.7 %copy-start.7 = (s32[8]{0:T(128)S(1)}, s32[8]{0:T(128)}, u32[]{:S(2)}) copy-start(s32[8]{0:T(128)} %lengths.1) | copy-start | bytes 100
  8.3 13.3 %copy-start = (bf16[1792,3584]{1,0:T(8,128)(2,1)S(1)}, bf16[1792,3584]{1,0:T(8,128)(2,1)}, u32[]{:S(2)}) copy-start(bf16[1792,3584]{1,0:T(8,128)(2,1)} %weight.1) | copy-start | bytes 38535172
  15.0 5.8 %collective-permute-start.5 = (f32[4,2048]{1,0:T(4,128)S(1)}, f32[4,2048]{1,0:T(4,128)S(1)}, u32[]{:S(2)}, u32[]{:S(2)}) collective-permute-start(f32[4,2048]{1,0:T(4,128)S(1)} %attend.1.rest_0_), channel_id=1, source_target_pairs={{0,12},{4,8},{8,4},{12,0},{1,13},{5,9},{9,5},{13,1},{2,14},{6,10},... | collective-permute-start | bytes 98312 | tf_op jit(solution)/shard_map/ppermute | solution.py:33
  16.5 5.1 %collective-permute-start.4 = (f32[4,2048]{1,0:T(4,128)S(1)}, f32[4,2048]{1,0:T(4,128)S(1)}, u32[]{:S(2)}, u32[]{:S(2)}) collective-permute-start(f32[4,2048]{1,0:T(4,128)S(1)} %attend.1.rest_0_), channel_id=1, source_target_pairs={{0,8},{4,12},{8,0},{12,4},{1,9},{5,13},{9,1},{13,5},{2,10},{6,14},... | collective-permute-start | bytes 98312 | tf_op jit(solution)/shard_map/ppermute | solution.py:33
  16.5 5.2 %collective-permute-start.3 = (f32[4,2048]{1,0:T(4,128)S(1)}, f32[4,2048]{1,0:T(4,128)S(1)}, u32[]{:S(2)}, u32[]{:S(2)}) collective-permute-start(f32[4,2048]{1,0:T(4,128)S(1)} %attend.1.rest_0_), channel_id=1, source_target_pairs={{0,4},{4,0},{8,12},{12,8},{1,5},{5,1},{9,13},{13,9},{2,6},{6,2},{1... | collective-permute-start | bytes 98312 | tf_op jit(solution)/shard_map/ppermute | solution.py:33
  23.7 1.9 %collective-permute-start.6 = (f32[2,3584]{1,0:T(2,128)S(1)}, f32[2,3584]{1,0:T(2,128)S(1)}, u32[]{:S(2)}, u32[]{:S(2)}) collective-permute-start(f32[2,3584]{1,0:T(2,128)S(1)} %get-tuple-element.16), channel_id=1, source_target_pairs={{0,1},{1,0},{2,3},{3,2},{4,5},{5,4},{6,7},{7,6},{8,9},{9,8},{10,11... | collective-permute-start | bytes 86024 | tf_op jit(solution)/shard_map/ppermute | solution.py:33
  23.7 3.9 %collective-permute-start.7 = (f32[2,3584]{1,0:T(2,128)S(1)}, f32[2,3584]{1,0:T(2,128)S(1)}, u32[]{:S(2)}, u32[]{:S(2)}) collective-permute-start(f32[2,3584]{1,0:T(2,128)S(1)} %get-tuple-element.17), channel_id=1, source_target_pairs={{0,2},{1,3},{2,0},{3,1},{4,6},{5,7},{6,4},{7,5},{8,10},{9,11},{10,... | collective-permute-start | bytes 86024 | tf_op jit(solution)/shard_map/ppermute | solution.py:33
  25.2 3.3 %collective-permute-start.8 = (f32[2,3584]{1,0:T(2,128)S(1)}, f32[2,3584]{1,0:T(2,128)S(1)}, u32[]{:S(2)}, u32[]{:S(2)}) collective-permute-start(f32[2,3584]{1,0:T(2,128)S(1)} %get-tuple-element.18), channel_id=1, source_target_pairs={{0,3},{1,2},{2,1},{3,0},{4,7},{5,6},{6,5},{7,4},{8,11},{9,10},{10,... | collective-permute-start | bytes 86024 | tf_op jit(solution)/shard_map/ppermute | solution.py:33
